TPU v7x, 32 devices: a whole 2x2x4 slice. The times are simulated.
32 devices in a mesh: fsdp: 4 (over y, core), context: 4 (over z), tensor: 2 (over x).
Axes of the slice: x: 2, y: 2, z: 4, core: 2. Of those that a mesh axis runs over, the one named last changes fastest.
Arguments:
- tokens: bfloat16 [4, 1024, 1536], P('fsdp', 'context'), may hold values from -6 to 6
- positions: int32 [4, 1024], P('fsdp', 'context'), may hold values from 0 to 1023, as said below
- expert_ids: int32 [4, 1024, 8], P('fsdp', 'context'), may hold values from 0 to 23, all different within a row; in each aligned block of 256 rows (0 to 255, 256 to 511, ..., all dimensions but the last counted through in order) at most 128 rows name the same one
- norm1_gain: bfloat16 [1536], P('fsdp'), may hold values from 0.5 to 1.5
- w_query: bfloat16 [1536, 1536], P('fsdp', 'tensor'), may hold values from -1 to 1
- key_projection_weight: bfloat16 [1536, 512], P('fsdp', 'tensor'), may hold values from -1 to 1
- value_projection_weight: bfloat16 [1536, 512], P('fsdp', 'tensor'), may hold values from -0.15625 to 0.15625
- w_out: bfloat16 [1536, 1536], P('tensor', 'fsdp'), may hold values from -0.875 to 0.875
- norm2_gain: bfloat16 [1536], P('fsdp'), may hold values from 0.5 to 1.5
- w_router: bfloat16 [1536, 24], P('fsdp'), may hold values from -0.15625 to 0.15625
- w_gate: bfloat16 [24, 1536, 512], P('fsdp', None, 'tensor'), may hold values from -0.15625 to 0.15625
- w_up: bfloat16 [24, 1536, 512], P('fsdp', None, 'tensor'), may hold values from -0.15625 to 0.15625
- w_down: bfloat16 [24, 512, 1536], P('fsdp', 'tensor'), may hold values from -0.5 to 0.5
- grad_output: bfloat16 [4, 1024, 1536], P('fsdp', 'context'), may hold values from -6 to 6
Outputs:
- output: bfloat16 [4, 1024, 1536], P('fsdp', 'context')
- grad_tokens: bfloat16 [4, 1024, 1536], P('fsdp', 'context')
- grad_norm1_gain: float32 [1536], P('fsdp')
- grad_w_query: float32 [1536, 1536], P('fsdp', 'tensor')
- grad_w_key: float32 [1536, 512], P('fsdp', 'tensor')
- grad_w_value: float32 [1536, 512], P('fsdp', 'tensor')
- grad_w_out: float32 [1536, 1536], P('tensor', 'fsdp')
- grad_norm2_gain: float32 [1536], P('fsdp')
- grad_w_router: float32 [1536, 24], P('fsdp')
- grad_w_gate: float32 [24, 1536, 512], P('fsdp', None, 'tensor')
- grad_w_up: float32 [24, 1536, 512], P('fsdp', None, 'tensor')
- grad_w_down: float32 [24, 512, 1536], P('fsdp', 'tensor')
Inputs may be any that keep to these rules, and one draw needn't show every extreme that they name: `expert_ids`: within each aligned block of 256 tokens of a sequence no expert is named by more than 128 tokens, a bound that some block reaches; a token names 8 different experts. `positions`: each sequence begins at position 0; every later position is 0 or one more than the position before it; the first sequence never restarts.
All inputs are finite; a program needn't handle non-finite values.
Results may differ from a plain program's by a relative error of at most 0.022.
Values may be sent and summed in bfloat16 or wider, within the bound.
A program may use at most 384 MiB of HBM per device.

v0:
```python
import math

import jax
import jax.numpy as jnp
from jax import lax
from jax.sharding import PartitionSpec as P

HEAD_DIMENSION = 64
TOPK = 8
CAP = 128


norm_eps = 1e-06
masked_score = -1e30


def rms_scale(rows):
    return lax.rsqrt(jnp.mean(rows * rows, axis=-1, keepdims=True) + norm_eps)


def norm_backward(rows, scale, gain, grad_out):
    weighted = grad_out * gain
    cubed = scale * scale * scale
    grad_in = scale * weighted - rows * cubed * jnp.mean(weighted * rows, axis=-1, keepdims=True)
    return (grad_in, jnp.sum(grad_out * rows * scale, axis=0))


def rope_tables(place_ids, head_size):
    half = head_size // 2
    freq = jnp.exp(-math.log(10000.0) * 2.0 * jnp.arange(half, dtype=jnp.float32) / head_size)
    angle = place_ids.astype(jnp.float32)[:, None] * freq[None, :]
    return (jnp.cos(angle), jnp.sin(angle))


def apply_rotation(value_matrix, cosine_table, sine_table, sign):
    half = value_matrix.shape[-1] // 2
    first = value_matrix[..., :half]
    second = value_matrix[..., half:]
    cos_b = cosine_table[:, None, :]
    sin_b = sine_table[:, None, :] * sign
    return jnp.concatenate(
        [first * cos_b - second * sin_b, second * cos_b + first * sin_b], axis=-1
    )


def slot_table(routes, experts, capacity):
    flat = routes.reshape(-1)
    onehot = (flat[:, None] == jnp.arange(experts, dtype=jnp.int32)[None, :]).astype(jnp.int32)
    before = jnp.cumsum(onehot, axis=0) - onehot
    slots = jnp.sum(before * onehot, axis=1)
    place = flat * capacity + slots
    owners = jnp.arange(flat.shape[0], dtype=jnp.int32) // routes.shape[1] + 1
    owner = jnp.zeros((experts * capacity,), jnp.int32).at[place].set(owners)
    filled = owner > 0
    source = jnp.maximum(owner - 1, 0)
    return (place, source, filled)


def expert_pass(rows_in, cotangent, gate_w, up_w, down_w):
    gate_pre = jnp.einsum("ecd,edf->ecf", rows_in, gate_w, preferred_element_type=jnp.float32)
    up_pre = jnp.einsum("ecd,edf->ecf", rows_in, up_w, preferred_element_type=jnp.float32)
    sigma = jax.nn.sigmoid(gate_pre)
    activated = gate_pre * sigma
    inner_b = (activated * up_pre).astype(jnp.bfloat16)
    expert_out = jnp.einsum("ecf,efd->ecd", inner_b, down_w, preferred_element_type=jnp.float32)
    grad_inner = jnp.einsum("ecd,efd->ecf", cotangent, down_w, preferred_element_type=jnp.float32)
    grad_down_w = jnp.einsum("ecf,ecd->efd", inner_b, cotangent, preferred_element_type=jnp.float32)
    grad_g = (grad_inner * up_pre * sigma * (1.0 + gate_pre * (1.0 - sigma))).astype(jnp.bfloat16)
    grad_u = (grad_inner * activated).astype(jnp.bfloat16)
    grad_disp = jnp.einsum("ecf,edf->ecd", grad_g, gate_w, preferred_element_type=jnp.float32)
    grad_disp = grad_disp + jnp.einsum(
        "ecf,edf->ecd", grad_u, up_w, preferred_element_type=jnp.float32
    )
    grad_gate_w = jnp.einsum("ecd,ecf->edf", rows_in, grad_g, preferred_element_type=jnp.float32)
    grad_up_w = jnp.einsum("ecd,ecf->edf", rows_in, grad_u, preferred_element_type=jnp.float32)
    return (expert_out, grad_disp, grad_gate_w, grad_up_w, grad_down_w)


def per_device(
    tokens,
    positions,
    expert_ids,
    norm1_gain,
    w_query,
    key_projection_weight,
    value_projection_weight,
    w_out,
    norm2_gain,
    w_router,
    w_gate,
    w_up,
    w_down,
    grad_output,
):
    weights = (
        lax.all_gather(norm1_gain, "fsdp", axis=0, tiled=True),
        lax.all_gather(w_query, "fsdp", axis=0, tiled=True),
        lax.all_gather(key_projection_weight, "fsdp", axis=0, tiled=True),
        lax.all_gather(value_projection_weight, "fsdp", axis=0, tiled=True),
        lax.all_gather(w_out, "fsdp", axis=1, tiled=True),
        lax.all_gather(norm2_gain, "fsdp", axis=0, tiled=True),
        lax.all_gather(w_router, "fsdp", axis=0, tiled=True),
        lax.all_gather(w_gate, "fsdp", axis=0, tiled=True),
        lax.all_gather(w_up, "fsdp", axis=0, tiled=True),
        lax.all_gather(w_down, "fsdp", axis=0, tiled=True),
    )
    gain_one_b, query_w, key_w, value_w, out_w, gain_two_b, router_w, gate_w, up_w, down_w = weights
    rows = tokens[0].astype(jnp.float32)
    block_len = rows.shape[0]
    heads_here = query_w.shape[1] // HEAD_DIMENSION
    groups_here = key_w.shape[1] // HEAD_DIMENSION
    group_repeat = heads_here // groups_here
    softmax_scale = 1.0 / math.sqrt(HEAD_DIMENSION)
    scale_one = rms_scale(rows)
    first_normalized = (rows * scale_one * gain_one_b.astype(jnp.float32)).astype(jnp.bfloat16)
    cosine_table, sine_table = rope_tables(positions[0], HEAD_DIMENSION)
    query_rows = apply_rotation(
        jnp.dot(first_normalized, query_w, preferred_element_type=jnp.float32).reshape(
            block_len, heads_here, HEAD_DIMENSION
        ),
        cosine_table,
        sine_table,
        1.0,
    ).astype(jnp.bfloat16)
    key_row_list = (
        apply_rotation(
            jnp.dot(first_normalized, key_w, preferred_element_type=jnp.float32).reshape(
                block_len, groups_here, HEAD_DIMENSION
            ),
            cosine_table,
            sine_table,
            1.0,
        )
        .astype(jnp.bfloat16)
        .reshape(block_len, groups_here * HEAD_DIMENSION)
    )
    value_row_list = jnp.dot(first_normalized, value_w, preferred_element_type=jnp.float32).astype(
        jnp.bfloat16
    )
    query_fourdim = query_rows.reshape(block_len, groups_here, group_repeat, HEAD_DIMENSION)
    query_pos = lax.axis_index("context") * block_len + jnp.arange(block_len, dtype=jnp.int32)
    start_state = (
        jnp.full((groups_here, group_repeat, block_len), masked_score, jnp.float32),
        jnp.zeros((groups_here, group_repeat, block_len), jnp.float32),
        jnp.zeros((block_len, groups_here, group_repeat, HEAD_DIMENSION), jnp.float32),
    )
    state = start_state
    key_piece = lax.all_gather(key_row_list, "context", axis=0, tiled=True)
    value_piece = lax.all_gather(value_row_list, "context", axis=0, tiled=True)
    sequence_length = key_piece.shape[0]
    width = math.gcd(sequence_length, 512)
    key_blocks = key_piece.reshape(sequence_length // width, width, groups_here, HEAD_DIMENSION)
    value_blocks = value_piece.reshape(sequence_length // width, width, groups_here, HEAD_DIMENSION)
    firsts = jnp.arange(sequence_length // width, dtype=jnp.int32) * width

    def attend_inner(carry, item):
        top, total, running_total = carry
        key_block_tile, value_block_tile, first = item
        score_matrix = (
            jnp.einsum(
                "ijzq,pjq->jzip", query_fourdim, key_block_tile, preferred_element_type=jnp.float32
            )
            * softmax_scale
        )
        allowed = (first + jnp.arange(width, dtype=jnp.int32))[None, :] <= query_pos[:, None]
        score_matrix = jnp.where(allowed, score_matrix, masked_score)
        new_top = jnp.maximum(top, jnp.max(score_matrix, axis=-1))
        exponent_values = jnp.where(allowed, jnp.exp(score_matrix - new_top[..., None]), 0.0)
        shrink = jnp.exp(top - new_top)
        total = total * shrink + jnp.sum(exponent_values, axis=-1)
        update = jnp.einsum(
            "hevu,uhw->vhew",
            exponent_values.astype(jnp.bfloat16),
            value_block_tile,
            preferred_element_type=jnp.float32,
        )
        running_total = running_total * jnp.transpose(shrink, (2, 0, 1))[..., None] + update
        return ((new_top, total, running_total), None)

    state, _ = lax.scan(attend_inner, state, (key_blocks, value_blocks, firsts))
    top, total, running_total = state
    attended = running_total / jnp.transpose(total, (2, 0, 1))[..., None]
    logsumexp_total = top + jnp.log(total)
    attended_batch = attended.astype(jnp.bfloat16).reshape(block_len, heads_here * HEAD_DIMENSION)
    mixed = lax.psum(jnp.dot(attended_batch, out_w, preferred_element_type=jnp.float32), "tensor")
    hidden = rows + mixed
    scale_two = rms_scale(hidden)
    normed_two = (hidden * scale_two * gain_two_b.astype(jnp.float32)).astype(jnp.bfloat16)
    experts = router_w.shape[1]
    logits = jnp.dot(normed_two, router_w, preferred_element_type=jnp.float32)
    routes = expert_ids[0]
    chooser = (routes[:, :, None] == jnp.arange(experts, dtype=jnp.int32)[None, None, :]).astype(
        jnp.float32
    )
    chosen = jnp.sum(chooser * logits[:, None, :], axis=-1)
    gates = jax.nn.softmax(chosen, axis=-1)
    place, source, filled = slot_table(routes, experts, CAP)
    grad_rows_out = grad_output[0].astype(jnp.float32)
    dispatched = jnp.where(
        filled[:, None], normed_two[source], jnp.zeros((), jnp.bfloat16)
    ).reshape(experts, CAP, -1)
    slot_gate = jnp.zeros((experts * CAP,), jnp.float32).at[place].set(gates.reshape(-1))
    grad_expert = (
        jnp.where(filled[:, None], grad_rows_out[source] * slot_gate[:, None], 0.0)
        .astype(jnp.bfloat16)
        .reshape(experts, CAP, -1)
    )
    expert_out, grad_disp, grad_gate_w, grad_up_w, grad_down_w = expert_pass(
        dispatched, grad_expert, gate_w, up_w, down_w
    )
    picked = expert_out.reshape(experts * CAP, -1)[place].reshape(block_len, TOPK, -1)
    moe_part = jnp.sum(gates[:, :, None] * picked, axis=1)
    grad_gates_part = jnp.sum(picked * grad_rows_out[:, None, :], axis=-1)
    grad_normed_part = jnp.sum(
        grad_disp.reshape(experts * CAP, -1)[place].reshape(block_len, TOPK, -1), axis=1
    )
    moe, grad_gates, grad_normed_e = (
        lax.psum(moe_part.astype(jnp.bfloat16), "tensor").astype(jnp.float32),
        lax.psum(grad_gates_part.astype(jnp.bfloat16), "tensor").astype(jnp.float32),
        lax.psum(grad_normed_part.astype(jnp.bfloat16), "tensor").astype(jnp.float32),
    )
    output = (hidden + moe).astype(jnp.bfloat16)
    grad_chosen = gates * (grad_gates - jnp.sum(gates * grad_gates, axis=-1, keepdims=True))
    grad_logits = jnp.sum(grad_chosen[:, :, None] * chooser, axis=1).astype(jnp.bfloat16)
    grad_normed_two = grad_normed_e + jnp.dot(
        grad_logits, router_w.T, preferred_element_type=jnp.float32
    )
    grad_router = jnp.dot(normed_two.T, grad_logits, preferred_element_type=jnp.float32)
    grad_hidden_n, grad_gain_two = norm_backward(
        hidden, scale_two, gain_two_b.astype(jnp.float32), grad_normed_two
    )
    grad_hidden = grad_rows_out + grad_hidden_n
    grad_hidden_b = grad_hidden.astype(jnp.bfloat16)
    attended_gradient = jnp.dot(grad_hidden_b, out_w.T, preferred_element_type=jnp.float32).astype(
        jnp.bfloat16
    )
    grad_out_w = jnp.dot(attended_batch.T, grad_hidden_b, preferred_element_type=jnp.float32)
    gradient_fourdim = attended_gradient.reshape(
        block_len, groups_here, group_repeat, HEAD_DIMENSION
    )
    delta = jnp.transpose(
        jnp.sum(
            gradient_fourdim.astype(jnp.float32)
            * attended_batch.reshape(block_len, groups_here, group_repeat, HEAD_DIMENSION).astype(
                jnp.float32
            ),
            axis=-1,
        ),
        (1, 2, 0),
    )
    grad_q = jnp.zeros((block_len, groups_here, group_repeat, HEAD_DIMENSION), jnp.float32)
    key_piece = lax.all_gather(key_row_list, "context", axis=0, tiled=True)
    value_piece = lax.all_gather(value_row_list, "context", axis=0, tiled=True)
    sequence_length = key_piece.shape[0]
    back_width = math.gcd(sequence_length, 512)
    key_blocks = key_piece.reshape(
        sequence_length // back_width, back_width, groups_here, HEAD_DIMENSION
    )
    value_blocks = value_piece.reshape(
        sequence_length // back_width, back_width, groups_here, HEAD_DIMENSION
    )
    firsts = jnp.arange(sequence_length // back_width, dtype=jnp.int32) * back_width

    def back_inner(grad_acc, item):
        key_block_tile, value_block_tile, first = item
        score_matrix = (
            jnp.einsum(
                "ijzq,pjq->jzip", query_fourdim, key_block_tile, preferred_element_type=jnp.float32
            )
            * softmax_scale
        )
        allowed = (first + jnp.arange(back_width, dtype=jnp.int32))[None, :] <= query_pos[:, None]
        probabilities = jnp.where(allowed, jnp.exp(score_matrix - logsumexp_total[..., None]), 0.0)
        grad_v_blk = jnp.einsum(
            "ihne,nihf->eif",
            probabilities.astype(jnp.bfloat16),
            gradient_fourdim,
            preferred_element_type=jnp.float32,
        )
        probability_gradient = jnp.einsum(
            "ijzq,pjq->jzip", gradient_fourdim, value_block_tile, preferred_element_type=jnp.float32
        )
        score_gradient = (probabilities * (probability_gradient - delta[..., None])).astype(
            jnp.bfloat16
        )
        grad_acc = (
            grad_acc
            + jnp.einsum(
                "hevu,uhw->vhew", score_gradient, key_block_tile, preferred_element_type=jnp.float32
            )
            * softmax_scale
        )
        grad_k_blk = (
            jnp.einsum(
                "ihne,nihf->eif", score_gradient, query_fourdim, preferred_element_type=jnp.float32
            )
            * softmax_scale
        )
        joined = jnp.concatenate(
            [grad_k_blk.reshape(back_width, -1), grad_v_blk.reshape(back_width, -1)], axis=1
        )
        return (grad_acc, joined)

    grad_q, joined_all = lax.scan(back_inner, grad_q, (key_blocks, value_blocks, firsts))
    grad_kv = joined_all.reshape(sequence_length, -1)
    grad_q, grad_kv = (grad_q, grad_kv)
    own_kv = lax.psum_scatter(
        grad_kv.astype(jnp.bfloat16), "context", scatter_dimension=0, tiled=True
    ).astype(jnp.float32)
    grad_queries = (
        apply_rotation(
            grad_q.reshape(block_len, heads_here, HEAD_DIMENSION), cosine_table, sine_table, -1.0
        )
        .astype(jnp.bfloat16)
        .reshape(block_len, -1)
    )
    key_rows_gradient = (
        apply_rotation(
            own_kv[:, : groups_here * HEAD_DIMENSION].reshape(
                block_len, groups_here, HEAD_DIMENSION
            ),
            cosine_table,
            sine_table,
            -1.0,
        )
        .astype(jnp.bfloat16)
        .reshape(block_len, -1)
    )
    value_rows_gradient = own_kv[:, groups_here * HEAD_DIMENSION :].astype(jnp.bfloat16)
    grad_normed_part_one = jnp.dot(grad_queries, query_w.T, preferred_element_type=jnp.float32)
    grad_normed_part_one = grad_normed_part_one + jnp.dot(
        key_rows_gradient, key_w.T, preferred_element_type=jnp.float32
    )
    grad_normed_part_one = grad_normed_part_one + jnp.dot(
        value_rows_gradient, value_w.T, preferred_element_type=jnp.float32
    )
    grad_normed_one = lax.psum(grad_normed_part_one.astype(jnp.bfloat16), "tensor").astype(
        jnp.float32
    )
    grad_query_w = jnp.dot(first_normalized.T, grad_queries, preferred_element_type=jnp.float32)
    grad_key_w = jnp.dot(first_normalized.T, key_rows_gradient, preferred_element_type=jnp.float32)
    grad_value_w = jnp.dot(
        first_normalized.T, value_rows_gradient, preferred_element_type=jnp.float32
    )
    grad_rows_n, grad_gain_one = norm_backward(
        rows, scale_one, gain_one_b.astype(jnp.float32), grad_normed_one
    )
    grad_tokens = (grad_hidden + grad_rows_n).astype(jnp.bfloat16)
    parts = (
        lax.psum_scatter(
            grad_gain_one.astype(jnp.bfloat16), "fsdp", scatter_dimension=0, tiled=True
        ).astype(jnp.float32),
        lax.psum_scatter(
            grad_query_w.astype(jnp.bfloat16), "fsdp", scatter_dimension=0, tiled=True
        ).astype(jnp.float32),
        lax.psum_scatter(
            grad_key_w.astype(jnp.bfloat16), "fsdp", scatter_dimension=0, tiled=True
        ).astype(jnp.float32),
        lax.psum_scatter(
            grad_value_w.astype(jnp.bfloat16), "fsdp", scatter_dimension=0, tiled=True
        ).astype(jnp.float32),
        lax.psum_scatter(
            grad_out_w.astype(jnp.bfloat16), "fsdp", scatter_dimension=1, tiled=True
        ).astype(jnp.float32),
        lax.psum_scatter(
            grad_gain_two.astype(jnp.bfloat16), "fsdp", scatter_dimension=0, tiled=True
        ).astype(jnp.float32),
        lax.psum_scatter(
            grad_router.astype(jnp.bfloat16), "fsdp", scatter_dimension=0, tiled=True
        ).astype(jnp.float32),
        lax.psum_scatter(
            grad_gate_w.astype(jnp.bfloat16), "fsdp", scatter_dimension=0, tiled=True
        ).astype(jnp.float32),
        lax.psum_scatter(
            grad_up_w.astype(jnp.bfloat16), "fsdp", scatter_dimension=0, tiled=True
        ).astype(jnp.float32),
        lax.psum_scatter(
            grad_down_w.astype(jnp.bfloat16), "fsdp", scatter_dimension=0, tiled=True
        ).astype(jnp.float32),
    )
    summed = (
        lax.psum(parts[0].astype(jnp.bfloat16), "context").astype(jnp.float32),
        lax.psum(parts[1].astype(jnp.bfloat16), "context").astype(jnp.float32),
        lax.psum(parts[2].astype(jnp.bfloat16), "context").astype(jnp.float32),
        lax.psum(parts[3].astype(jnp.bfloat16), "context").astype(jnp.float32),
        lax.psum(parts[4].astype(jnp.bfloat16), "context").astype(jnp.float32),
        lax.psum(parts[5].astype(jnp.bfloat16), "context").astype(jnp.float32),
        lax.psum(parts[6].astype(jnp.bfloat16), "context").astype(jnp.float32),
        lax.psum(parts[7].astype(jnp.bfloat16), "context").astype(jnp.float32),
        lax.psum(parts[8].astype(jnp.bfloat16), "context").astype(jnp.float32),
        lax.psum(parts[9].astype(jnp.bfloat16), "context").astype(jnp.float32),
    )
    return (
        output[None],
        grad_tokens[None],
        summed[0],
        summed[1],
        summed[2],
        summed[3],
        summed[4],
        summed[5],
        summed[6],
        summed[7],
        summed[8],
        summed[9],
    )


def solution(mesh):
    return jax.shard_map(
        per_device,
        mesh=mesh,
        in_specs=(
            P("fsdp", "context", None),
            P("fsdp", "context"),
            P("fsdp", "context", None),
            P("fsdp"),
            P("fsdp", "tensor"),
            P("fsdp", "tensor"),
            P("fsdp", "tensor"),
            P("tensor", "fsdp"),
            P("fsdp"),
            P("fsdp", None),
            P("fsdp", None, "tensor"),
            P("fsdp", None, "tensor"),
            P("fsdp", "tensor", None),
            P("fsdp", "context", None),
        ),
        out_specs=(
            P("fsdp", "context", None),
            P("fsdp", "context", None),
            P("fsdp"),
            P("fsdp", "tensor"),
            P("fsdp", "tensor"),
            P("fsdp", "tensor"),
            P("tensor", "fsdp"),
            P("fsdp"),
            P("fsdp", None),
            P("fsdp", None, "tensor"),
            P("fsdp", None, "tensor"),
            P("fsdp", "tensor", None),
        ),
        check_vma=False,
    )
```

profile of v0, /device:TPU:0, one launch (start us, length us, event | category | flops | bytes accessed | tf_op | source)
XLA Modules:
  0.0 1928.4 jit_solution(5089044217878180472)
XLA Ops:
  34.3 16.5 all_gather.40
  68.2 16.6 all_gather.43
  92.8 26.3 %while.28 = (s32[]{:T(128)}, f32[4,3,256]{2,1,0:T(4,128)S(1)}, f32[4,3,256]{2,1,0:T(4,128)S(1)}, f32[256,4,3,64]{0,3,2,1:T(8,128)S(1)}, s32[2]{0:T(128)}, /*inde...) while((s32[]{:T(128)}, f32[4,3,256]{2,1,0:T(4,128)S(1)}, ...), condition=%wide.region_4.5_spmd.clone, body=%wide.region_1.4_spmd.clone.sunk | while | flops 423840512 | bytes 40975040 | solution.py:180
  147.4 15.9 gather_fusion.2
  203.3 94.5 %all-gather.14.cloned.1.call-done = bf16[24,1536,256]{2,1,0:T(8,128)(2,1)} async-done(((bf16[6,1536,256]{2,1,0:T(8,128)(2,1)}), bf16[24,1536,256]{2,1,0:T(8,128)(2,1)}) %all-gather.14.cloned.1.call-update) | async-done | bytes 18874384 | tf_op jit(solution)/shard_map/all_gather | solution.py:104
  312.3 107.0 %all-gather.12.cloned.1.call-done = bf16[24,1536,256]{2,1,0:T(8,128)(2,1)} async-done(((bf16[6,1536,256]{2,1,0:T(8,128)(2,1)}), bf16[24,1536,256]{2,1,0:T(8,128)(2,1)}) %all-gather.12.cloned.1.call-update) | async-done | bytes 18874384 | tf_op jit(solution)/shard_map/all_gather | solution.py:103
  433.7 107.1 %all-gather.16.cloned.1.call-done = bf16[24,256,1536]{2,1,0:T(8,128)(2,1)} async-done(((bf16[6,256,1536]{2,1,0:T(8,128)(2,1)}), bf16[24,256,1536]{2,1,0:T(8,128)(2,1)}) %all-gather.16.cloned.1.call-update) | async-done | bytes 18874384 | tf_op jit(solution)/shard_map/all_gather | solution.py:105
  540.7 17.6 multiply_convert_fusion
  573.1 21.2 %convolution_add_fusion = f32[24,128,1536]{2,1,0:T(8,128)} fusion(f32[24,128,1536]{2,1,0:T(8,128)} %fusion.127, bf16[24,128,256]{2,1,0:T(8,128)(2,1)S(1)} %get-tuple-element.362, bf16[24,1536,256]{2,1,0:T(8,128)(2,1)} %all-gather.14.cloned.1.call-done), kind=kOutput, calls=%fused_computation.77 | convolution fusion | flops 2420637696 | bytes 58195968 | tf_op jit(solution)/shard_map/ecf,edf->ecd/dot_general | solution.py:71
  594.4 20.6 %gather_fusion.3 = f32[2048,1536]{1,0:T(8,128)} fusion(f32[3072,1536]{1,0:T(8,128)} %bitcast.297, s32[2048]{0:T(1024)S(1)} %broadcast_clamp_fusion), kind=kCustom, calls=%fused_computation.3 | custom fusion | bytes 25174016 | tf_op jit(solution)/shard_map/gather | solution.py:215
  623.7 15.7 fusion.126
  639.3 20.9 %gather_fusion.1 = f32[2048,1536]{1,0:T(8,128)} fusion(f32[3072,1536]{1,0:T(8,128)} %bitcast.298, s32[2048]{0:T(1024)S(1)} %broadcast_clamp_fusion), kind=kCustom, calls=%fused_computation.1 | custom fusion | bytes 25174016 | tf_op jit(solution)/shard_map/gather | solution.py:211
  682.3 36.0 %while.29 = (s32[]{:T(128)}, f32[256,4,3,64]{0,3,2,1:T(8,128)}, bf16[2,512,512]{2,1,0:T(8,128)(2,1)}, bf16[2,512,4,64]{1,3,2,0:T(8,128)(2,1)}, s32[2]{0:T(128)},...) while((s32[]{:T(128)}, f32[256,4,3,64]{0,3,2,1:T(8,128)}, ...), condition=%wide.region_26.27_spmd.clone, body=%wide.region_25.26_spmd.clone.sunk | while | flops 1024393984 | bytes 38506196 | solution.py:304
  723.5 22.3 %reduce-scatter.14.cloned.1.call-done = bf16[256,512]{1,0:T(8,128)(2,1)} async-done(((bf16[1024,512]{1,0:T(8,128)(2,1)}), bf16[256,512]{1,0:T(8,128)(2,1)}) %reduce-scatter.14.cloned.1.call-update) | async-done | bytes 262160 | tf_op jit(solution)/shard_map/reduce_scatter | solution.py:307
  752.7 17.0 convolution_convert_fusion
  806.5 26.3 %reduce-scatter.20.cloned.1.call-done = bf16[384,256]{1,0:T(8,128)(2,1)} async-done(((bf16[1536,256]{1,0:T(8,128)(2,1)}), bf16[384,256]{1,0:T(8,128)(2,1)}) %reduce-scatter.20.cloned.1.call-update) | async-done | bytes 196624 | tf_op jit(solution)/shard_map/reduce_scatter | solution.py:359
  832.8 35.8 %reduce-scatter.16.cloned.1.call-done = bf16[384,768]{1,0:T(8,128)(2,1)} async-done(((bf16[1536,768]{1,0:T(8,128)(2,1)}), bf16[384,768]{1,0:T(8,128)(2,1)}) %reduce-scatter.16.cloned.1.call-update) | async-done | bytes 589840 | tf_op jit(solution)/shard_map/reduce_scatter | solution.py:353
  868.6 140.4 %reduce-scatter.26.cloned.1.call-done = bf16[6,256,1536]{2,1,0:T(8,128)(2,1)} async-done(((bf16[24,256,1536]{2,1,0:T(8,128)(2,1)}), bf16[6,256,1536]{2,1,0:T(8,128)(2,1)}) %reduce-scatter.26.cloned.1.call-update) | async-done | bytes 4718608 | tf_op jit(solution)/shard_map/reduce_scatter | solution.py:377
  1009.1 140.3 %reduce-scatter.22.cloned.1.call-done = bf16[6,1536,256]{2,1,0:T(8,128)(2,1)} async-done(((bf16[24,1536,256]{2,1,0:T(8,128)(2,1)}), bf16[6,1536,256]{2,1,0:T(8,128)(2,1)}) %reduce-scatter.22.cloned.1.call-update) | async-done | bytes 4718608 | tf_op jit(solution)/shard_map/reduce_scatter | solution.py:371
  1149.4 140.3 %reduce-scatter.24.cloned.1.call-done = bf16[6,1536,256]{2,1,0:T(8,128)(2,1)} async-done(((bf16[24,1536,256]{2,1,0:T(8,128)(2,1)}), bf16[6,1536,256]{2,1,0:T(8,128)(2,1)}) %reduce-scatter.24.cloned.1.call-update) | async-done | bytes 4718608 | tf_op jit(solution)/shard_map/reduce_scatter | solution.py:374
  1291.6 21.9 %reduce-scatter.30.cloned.1.call-done = bf16[384,24]{1,0:T(8,128)(2,1)} async-done(((bf16[1536,24]{1,0:T(8,128)(2,1)}), bf16[384,24]{1,0:T(8,128)(2,1)}) %reduce-scatter.30.cloned.1.call-update) | async-done | bytes 18448
  1314.4 53.4 %all-reduce.17.cloned.1.call-done = (bf16[256,1536]{1,0:T(8,128)(2,1)}, bf16[256,1536]{1,0:T(8,128)(2,1)}) async-done(((bf16[256,1536]{1,0:T(8,128)(2,1)}, bf16[256,1536]{1,0:T(8,128)(2,1)}), (bf16[256,1536]{1,0:T(8,128)(2,1)}, bf16[256,1536]{1,0:T(8,128)(2,1)})) %all-reduce.17.cloned.1.call-update) | async-done | bytes 1572880 | tf_op jit(solution)/shard_map/psum | solution.py:218
  1376.4 27.2 %all-reduce.2 = (bf16[384]{0:T(512)(128)(2,1)S(1)}, bf16[384]{0:T(512)(128)(2,1)S(1)}, bf16[384,24]{0,1:T(8,128)(2,1)S(1)}) all-reduce(bf16[384]{0:T(512)(128)(2,1)S(1)} %dynamic-slice.1, bf16[384]{0:T(512)(128)(2,1)S(1)} %dynamic-slice.3, bf16[384,24]{0,1:T(8,128)(2,1)S(1)} %copy.155), channel_id=1, replica_groups=mesh['fsdp'=4,'context'=4,'tensor'=2] {'context'}, use_global_device_ids=true, to_apply=%region_32.33 | all-reduce | flops 9984 | bytes 39936 | tf_op jit(solution)/shard_map/psum | solution.py:382
  1408.7 491.6 %all-reduce.15.cloned.1.call-done = (bf16[384,768]{1,0:T(8,128)(2,1)}, bf16[384,256]{1,0:T(8,128)(2,1)}, bf16[384,256]{1,0:T(8,128)(2,1)}, bf16[768,384]{1,0:T(8...) async-done(((bf16[384,768]{1,0:T(8,128)(2,1)}, bf16[384,256]{1,0:T(8,128)(2,1)}, ...) | async-done | bytes 15728656 | tf_op jit(solution)/shard_map/psum | solution.py:383
  (388 shorter events, 341.4 us)
Async XLA Ops:
  7.2 78.6 %all-gather.8.cloned.1.call-start = ((), (), s32[]{:S(2)}) async-start(), calls=%async_computation.9 | async-start | bytes 2949120 | tf_op jit(solution)/shard_map/all_gather | solution.py:97
  7.9 111.4 %all-gather.10.cloned.1.call-start = ((), (), s32[]{:S(2)}) async-start(), calls=%async_computation.10 | async-start | bytes 2949120 | tf_op jit(solution)/shard_map/all_gather | solution.py:100
  8.7 167.7 %all-reduce.11.cloned.1.call-start = ((), (), s32[]{:S(2)}) async-start(), calls=%async_computation.11 | async-start | bytes 3145728 | tf_op jit(solution)/shard_map/psum | solution.py:185
  123.6 174.3 %all-gather.14.cloned.1.call-start = ((), (), s32[]{:S(2)}) async-start(), calls=%async_computation.13 | async-start | bytes 23592960 | tf_op jit(solution)/shard_map/all_gather | solution.py:104
  124.1 295.1 %all-gather.12.cloned.1.call-start = ((), (), s32[]{:S(2)}) async-start(), calls=%async_computation.12 | async-start | bytes 23592960 | tf_op jit(solution)/shard_map/all_gather | solution.py:103
  124.8 416.0 %all-gather.16.cloned.1.call-start = ((), (), s32[]{:S(2)}) async-start(), calls=%async_computation.14 | async-start | bytes 23592960 | tf_op jit(solution)/shard_map/all_gather | solution.py:105
  125.3 549.5 %all-reduce.13.cloned.1.call-start = ((), (), s32[]{:S(2)}) async-start(), calls=%async_computation.15 | async-start | bytes 1572864 | tf_op jit(solution)/shard_map/psum | solution.py:220
  168.6 372.1 %copy-start.51 = (pred[24,128]{1,0:T(8,128)(4,1)}, pred[24,128]{1,0:T(8,128)(4,1)S(1)}, u32[]{:S(2)}) copy-start(pred[24,128]{1,0:T(8,128)(4,1)S(1)} %compare_bitcast_fusion) | copy-start | bytes 9220
  194.4 117.8 %copy-start.65 = (f32[256]{0:T(256)}, f32[256]{0:T(256)S(1)}, u32[]{:S(2)}) copy-start(f32[256]{0:T(256)S(1)} %reduce_max.18) | copy-start | bytes 3076
  195.0 117.3 %copy-start.70 = (f32[256]{0:T(256)}, f32[256]{0:T(256)S(1)}, u32[]{:S(2)}) copy-start(f32[256]{0:T(256)S(1)} %fusion.106) | copy-start | bytes 3076
  195.1 117.1 %copy-start.32 = (f32[256,8]{1,0:T(8,128)}, f32[256,8]{1,0:T(8,128)S(1)}, u32[]{:S(2)}) copy-start(f32[256,8]{1,0:T(8,128)S(1)} %copy.122) | copy-start | bytes 24580
  203.3 337.4 %copy-start.62 = (f32[3072]{0:T(1024)}, f32[3072]{0:T(1024)S(1)}, u32[]{:S(2)}) copy-start(f32[3072]{0:T(1024)S(1)} %scatter_custom_fusion.1) | copy-start | bytes 36868
  623.6 122.2 %reduce-scatter.14.cloned.1.call-start = ((), (), s32[]{:S(2)}) async-start(), calls=%async_computation.16 | async-start | bytes 1310720 | tf_op jit(solution)/shard_map/reduce_scatter | solution.py:307
  718.4 84.9 %reduce-scatter.28.cloned.1.call-start = ((), (), s32[]{:S(2)}) async-start(), calls=%async_computation.23 | async-start | bytes 2949120
  723.2 83.3 %reduce-scatter.18.cloned.1.call-start = ((), (), s32[]{:S(2)}) async-start(), calls=%async_computation.18 | async-start | bytes 983040 | tf_op jit(solution)/shard_map/reduce_scatter | solution.py:356
  748.5 84.3 %reduce-scatter.20.cloned.1.call-start = ((), (), s32[]{:S(2)}) async-start(), calls=%async_computation.19 | async-start | bytes 983040 | tf_op jit(solution)/shard_map/reduce_scatter | solution.py:359
  750.0 118.7 %reduce-scatter.16.cloned.1.call-start = ((), (), s32[]{:S(2)}) async-start(), calls=%async_computation.17 | async-start | bytes 2949120 | tf_op jit(solution)/shard_map/reduce_scatter | solution.py:353
  752.6 256.5 %reduce-scatter.26.cloned.1.call-start = ((), (), s32[]{:S(2)}) async-start(), calls=%async_computation.22 | async-start | bytes 23592960 | tf_op jit(solution)/shard_map/reduce_scatter | solution.py:377
  769.7 379.7 %reduce-scatter.22.cloned.1.call-start = ((), (), s32[]{:S(2)}) async-start(), calls=%async_computation.20 | async-start | bytes 23592960 | tf_op jit(solution)/shard_map/reduce_scatter | solution.py:371
  782.7 507.0 %reduce-scatter.24.cloned.1.call-start = ((), (), s32[]{:S(2)}) async-start(), calls=%async_computation.21 | async-start | bytes 23592960 | tf_op jit(solution)/shard_map/reduce_scatter | solution.py:374
  795.6 517.9 %reduce-scatter.30.cloned.1.call-start = ((), (), s32[]{:S(2)}) async-start(), calls=%async_computation.24 | async-start | bytes 491520
  800.2 567.6 %all-reduce.17.cloned.1.call-start = ((), (), s32[]{:S(2)}) async-start(), calls=%async_computation.26 | async-start | bytes 3145728 | tf_op jit(solution)/shard_map/psum | solution.py:218
  802.9 1097.5 %all-reduce.15.cloned.1.call-start = ((), (), s32[]{:S(2)}) async-start(), calls=%async_computation.25 | async-start | bytes 31457280 | tf_op jit(solution)/shard_map/psum | solution.py:383
  1289.7 115.6 %copy-start.76 = (f32[256]{0:T(256)S(1)}, f32[256]{0:T(256)}, u32[]{:S(2)}) copy-start(f32[256]{0:T(256)} %get-tuple-element.376) | copy-start | bytes 3076
  (82 other events, 1272.4 us)
Sparse Core Ops, SparseCore 0:
  9.6 30.9 all-gather.7
  42.1 28.2 all-gather.9
  123.6 52.6 all-reduce.10
  177.8 119.9 all-gather.13
  299.3 119.9 all-gather.11
  420.7 119.9 all-gather.15
  623.7 34.3 all-reduce.12
  718.5 27.2 reduce-scatter.13
  748.9 31.2 reduce-scatter.27
  783.2 23.2 reduce-scatter.17
  809.6 23.1 reduce-scatter.19
  835.8 32.8 reduce-scatter.15
  871.2 137.8 reduce-scatter.25
  1011.5 137.8 reduce-scatter.21
  1151.8 137.8 reduce-scatter.23
  1292.6 20.8 reduce-scatter.29
  1316.3 51.5 all-reduce.16
  1371.7 528.6 all-reduce.14
where the time goes:
time: 1940 us; the launch traced here: 1930 us
  waiting for transfers between devices  1390 us (72%)
  matrix products  202 us (10%)
  local copies, waits for them, and re-layouts  129 us (7%)
  blocking collectives  116 us (6%)
  other arithmetic  71.4 us (4%)
    psum x1, waiting for transfers between devices, per_device(): lax.psum(parts[1].astype(jnp.bfloat16), 'context').astype(jnp.float32)  492 us
    reduce_scatter x1, waiting for transfers between devices, per_device(): lax.psum_scatter(grad_down_w.astype(jnp.bfloat16), 'fsdp', scatter_dimens...  140 us
    reduce_scatter x1, waiting for transfers between devices, per_device(): lax.psum_scatter(grad_gate_w.astype(jnp.bfloat16), 'fsdp', scatter_dimens...  140 us
    reduce_scatter x1, waiting for transfers between devices, per_device(): lax.psum_scatter(grad_up_w.astype(jnp.bfloat16), 'fsdp', scatter_dimensio...  140 us
    all_gather x1, waiting for transfers between devices, per_device(): lax.all_gather(w_down, 'fsdp', axis=0, tiled=True)  107 us
    all_gather x1, waiting for transfers between devices, per_device(): lax.all_gather(w_gate, 'fsdp', axis=0, tiled=True)  107 us
    all_gather x1, waiting for transfers between devices, per_device(): lax.all_gather(w_up, 'fsdp', axis=0, tiled=True)  94.5 us
    psum x1, waiting for transfers between devices, per_device(): lax.psum(moe_part.astype(jnp.bfloat16), 'tensor').astype(jnp.float32)  53.4 us
  transfers between devices with their start and end apart: 18, of which 14 were waited for; matrix products, arithmetic and copies ran while one was open for 13% of the time, Pallas kernels for 0%

commit v1 on v0

--- a/solution.py
+++ b/solution.py
@@ -3,6 +3,8 @@
 import jax
 import jax.numpy as jnp
 from jax import lax
+from jax.experimental import pallas as pl
+from jax.experimental.pallas import tpu as pltpu
 from jax.sharding import PartitionSpec as P
 
 HEAD_DIMENSION = 64
@@ -43,37 +45,276 @@
     )
 
 
-def slot_table(routes, experts, capacity):
-    flat = routes.reshape(-1)
-    onehot = (flat[:, None] == jnp.arange(experts, dtype=jnp.int32)[None, :]).astype(jnp.int32)
-    before = jnp.cumsum(onehot, axis=0) - onehot
-    slots = jnp.sum(before * onehot, axis=1)
-    place = flat * capacity + slots
-    owners = jnp.arange(flat.shape[0], dtype=jnp.int32) // routes.shape[1] + 1
-    owner = jnp.zeros((experts * capacity,), jnp.int32).at[place].set(owners)
-    filled = owner > 0
-    source = jnp.maximum(owner - 1, 0)
-    return (place, source, filled)
-
-
-def expert_pass(rows_in, cotangent, gate_w, up_w, down_w):
-    gate_pre = jnp.einsum("ecd,edf->ecf", rows_in, gate_w, preferred_element_type=jnp.float32)
-    up_pre = jnp.einsum("ecd,edf->ecf", rows_in, up_w, preferred_element_type=jnp.float32)
-    sigma = jax.nn.sigmoid(gate_pre)
+def nn(left, right):
+    return jnp.dot(left, right, preferred_element_type=jnp.float32)
+
+
+def nt(left, right):
+    return lax.dot_general(
+        left, right, (((1,), (1,)), ((), ())), preferred_element_type=jnp.float32
+    )
+
+
+def tn(left, right):
+    return lax.dot_general(
+        left, right, (((0,), (0,)), ((), ())), preferred_element_type=jnp.float32
+    )
+
+
+def dense_gates(normed, ids, router):
+    logits = nn(normed, router)
+    lanes = lax.broadcasted_iota(jnp.int32, logits.shape, 1)
+    mask = ids[:, 0:1] == lanes
+    for k in range(1, ids.shape[1]):
+        mask = mask | (ids[:, k : k + 1] == lanes)
+    logits = jnp.where(mask, logits, masked_score)
+    weight = jnp.where(mask, jnp.exp(logits - jnp.max(logits, axis=-1, keepdims=True)), 0.0)
+    return weight / jnp.sum(weight, axis=-1, keepdims=True)
+
+
+def gates_kernel(normed_ref, ids_ref, router_ref, gates_ref):
+    gates_ref[...] = dense_gates(normed_ref[...], ids_ref[...], router_ref[...])
+
+
+def gates_call(normed, ids, router):
+    rows, width = normed.shape
+    experts = router.shape[1]
+    tile = 1024
+    return pl.pallas_call(
+        gates_kernel,
+        out_shape=jax.ShapeDtypeStruct((rows, experts), jnp.float32),
+        grid=(rows // tile,),
+        in_specs=[
+            pl.BlockSpec((tile, width), lambda i: (i, 0)),
+            pl.BlockSpec((tile, ids.shape[1]), lambda i: (i, 0)),
+            pl.BlockSpec((width, experts), lambda i: (0, 0)),
+        ],
+        out_specs=pl.BlockSpec((tile, experts), lambda i: (i, 0)),
+        name="gates_all",
+        cost_estimate=pl.CostEstimate(
+            flops=2 * rows * width * 128, bytes_accessed=rows * width * 2, transcendentals=0
+        ),
+    )(normed, ids, router)
+
+
+def gate_column(gates, expert):
+    lanes = lax.broadcasted_iota(jnp.int32, gates.shape, 1)
+    return jnp.sum(jnp.where(lanes == expert, gates, 0.0), axis=-1, keepdims=True)
+
+
+def hidden_terms(normed, cotangent, gate_col, gate_w, up_w, down_w):
+    gate_pre = nn(normed, gate_w)
+    up_pre = nn(normed, up_w)
+    plain = nt(cotangent, down_w)
+    sigma = 1.0 / (1.0 + jnp.exp(-gate_pre))
     activated = gate_pre * sigma
-    inner_b = (activated * up_pre).astype(jnp.bfloat16)
-    expert_out = jnp.einsum("ecf,efd->ecd", inner_b, down_w, preferred_element_type=jnp.float32)
-    grad_inner = jnp.einsum("ecd,efd->ecf", cotangent, down_w, preferred_element_type=jnp.float32)
-    grad_down_w = jnp.einsum("ecf,ecd->efd", inner_b, cotangent, preferred_element_type=jnp.float32)
-    grad_g = (grad_inner * up_pre * sigma * (1.0 + gate_pre * (1.0 - sigma))).astype(jnp.bfloat16)
+    inner = activated * up_pre
+    grad_inner = gate_col * plain
+    scaled = (gate_col * inner).astype(jnp.bfloat16)
+    grad_g = (grad_inner * up_pre * (sigma + activated * (1.0 - sigma))).astype(jnp.bfloat16)
     grad_u = (grad_inner * activated).astype(jnp.bfloat16)
-    grad_disp = jnp.einsum("ecf,edf->ecd", grad_g, gate_w, preferred_element_type=jnp.float32)
-    grad_disp = grad_disp + jnp.einsum(
-        "ecf,edf->ecd", grad_u, up_w, preferred_element_type=jnp.float32
-    )
-    grad_gate_w = jnp.einsum("ecd,ecf->edf", rows_in, grad_g, preferred_element_type=jnp.float32)
-    grad_up_w = jnp.einsum("ecd,ecf->edf", rows_in, grad_u, preferred_element_type=jnp.float32)
-    return (expert_out, grad_disp, grad_gate_w, grad_up_w, grad_down_w)
+    return inner, plain, scaled, grad_g, grad_u
+
+
+def own_kernel(
+    first_ref,
+    normed_ref,
+    cot_ref,
+    ids_ref,
+    router_ref,
+    gate_hbm,
+    up_hbm,
+    down_hbm,
+    moe_ref,
+    grad_ref,
+    router_grad_ref,
+    gate_w,
+    up_w,
+    down_w,
+    all_inner,
+    all_g,
+    all_u,
+    gates,
+    gate_grads,
+    sems,
+):
+    experts_here = gate_w.shape[0]
+    hidden = gate_w.shape[2]
+    rows = normed_ref.shape[0]
+    tile = 256
+    for e in range(experts_here):
+        pltpu.make_async_copy(gate_hbm.at[e], gate_w.at[e], sems.at[0, e]).start()
+        pltpu.make_async_copy(up_hbm.at[e], up_w.at[e], sems.at[1, e]).start()
+        pltpu.make_async_copy(down_hbm.at[e], down_w.at[e], sems.at[2, e]).start()
+    first = first_ref[0]
+
+    def route(i, carry):
+        at = pl.ds(pl.multiple_of(i * tile, tile), tile)
+        gates[at, :] = dense_gates(normed_ref[at, :], ids_ref[at, :], router_ref[...])
+        gate_grads[at, :] = jnp.zeros((tile, gates.shape[1]), jnp.float32)
+        return carry
+
+    lax.fori_loop(0, rows // tile, route, 0)
+
+    def one_expert(e, carry):
+        pltpu.make_async_copy(gate_hbm.at[e], gate_w.at[e], sems.at[0, e]).wait()
+        pltpu.make_async_copy(up_hbm.at[e], up_w.at[e], sems.at[1, e]).wait()
+        pltpu.make_async_copy(down_hbm.at[e], down_w.at[e], sems.at[2, e]).wait()
+        columns = pl.ds(pl.multiple_of(e * hidden, hidden), hidden)
+
+        def one_tile(i, inner_carry):
+            at = pl.ds(pl.multiple_of(i * 512, 512), 512)
+            gates_tile = gates[at, :]
+            inner, plain, scaled, grad_g, grad_u = hidden_terms(
+                normed_ref[at, :],
+                cot_ref[at, :],
+                gate_column(gates_tile, first + e),
+                gate_w[e],
+                up_w[e],
+                down_w[e],
+            )
+            all_inner[at, columns] = scaled
+            all_g[at, columns] = grad_g
+            all_u[at, columns] = grad_u
+            share = jnp.sum(inner * plain, axis=-1, keepdims=True)
+            lanes = lax.broadcasted_iota(jnp.int32, gates_tile.shape, 1)
+            gate_grads[at, :] = jnp.where(lanes == first + e, share, gate_grads[at, :])
+            return inner_carry
+
+        lax.fori_loop(0, rows // 512, one_tile, 0)
+        return carry
+
+    lax.fori_loop(0, experts_here, one_expert, 0)
+
+    router_grad_ref[...] = jnp.zeros_like(router_grad_ref)
+
+    def finish(i, carry):
+        at = pl.ds(pl.multiple_of(i * tile, tile), tile)
+        gates_tile = gates[at, :]
+        grads_tile = gate_grads[at, :]
+        mean = jnp.sum(gates_tile * grads_tile, axis=-1, keepdims=True)
+        grad_logits = (gates_tile * (grads_tile - mean)).astype(jnp.bfloat16)
+        router_grad_ref[...] += tn(normed_ref[at, :], grad_logits)
+        down_all = down_w[...].reshape(experts_here * hidden, down_w.shape[2])
+        moe_ref[at, :] = nn(all_inner[at, :], down_all).astype(jnp.bfloat16)
+        total = nt(grad_logits, router_ref[...])
+        for e in range(experts_here):
+            columns = slice(e * hidden, (e + 1) * hidden)
+            total = total + nt(all_g[at, columns], gate_w[e]) + nt(all_u[at, columns], up_w[e])
+        grad_ref[at, :] = total.astype(jnp.bfloat16)
+        return carry
+
+    lax.fori_loop(0, rows // tile, finish, 0)
+
+
+def own_call(first, normed, cotangent, ids, router, gate_w, up_w, down_w):
+    rows, width = normed.shape
+    experts = router.shape[1]
+    here, _, hidden = gate_w.shape
+    vmem = pl.BlockSpec(memory_space=pltpu.VMEM)
+    anywhere = pl.BlockSpec(memory_space=pl.ANY)
+    return pl.pallas_call(
+        own_kernel,
+        out_shape=(
+            jax.ShapeDtypeStruct((rows, width), jnp.bfloat16),
+            jax.ShapeDtypeStruct((rows, width), jnp.bfloat16),
+            jax.ShapeDtypeStruct((width, experts), jnp.float32),
+        ),
+        in_specs=[pl.BlockSpec(memory_space=pltpu.SMEM)] + [vmem] * 4 + [anywhere] * 3,
+        out_specs=(vmem, vmem, vmem),
+        scratch_shapes=[
+            pltpu.VMEM(gate_w.shape, jnp.bfloat16),
+            pltpu.VMEM(up_w.shape, jnp.bfloat16),
+            pltpu.VMEM(down_w.shape, jnp.bfloat16),
+            pltpu.VMEM((rows, here * hidden), jnp.bfloat16),
+            pltpu.VMEM((rows, here * hidden), jnp.bfloat16),
+            pltpu.VMEM((rows, here * hidden), jnp.bfloat16),
+            pltpu.VMEM((rows, experts), jnp.float32),
+            pltpu.VMEM((rows, experts), jnp.float32),
+            pltpu.SemaphoreType.DMA((3, here)),
+        ],
+        compiler_params=pltpu.CompilerParams(vmem_limit_bytes=62 << 20),
+        name="experts_own",
+        cost_estimate=pl.CostEstimate(
+            flops=12 * rows * width * hidden * here,
+            bytes_accessed=6 * here * width * hidden + 8 * rows * width,
+            transcendentals=0,
+        ),
+    )(first, normed, cotangent, ids, router, gate_w, up_w, down_w)
+
+
+def weights_kernel(first_ref, *refs):
+    (normed_ref, cot_ref, gates_ref, gate_w, up_w, down_w) = refs[:6]
+    grad_gate_ref, grad_up_ref, grad_down_ref = refs[-3:]
+    e = pl.program_id(0)
+    normed = normed_ref[...]
+    cotangent = cot_ref[...]
+    _, _, scaled, grad_g, grad_u = hidden_terms(
+        normed,
+        cotangent,
+        gate_column(gates_ref[...], first_ref[0] + e),
+        gate_w[0],
+        up_w[0],
+        down_w[0],
+    )
+
+    @pl.when(pl.program_id(1) == 0)
+    def _():
+        grad_gate_ref[0] = tn(normed, grad_g)
+        grad_up_ref[0] = tn(normed, grad_u)
+        grad_down_ref[0] = tn(scaled, cotangent)
+
+    @pl.when(pl.program_id(1) > 0)
+    def _():
+        grad_gate_ref[0] += tn(normed, grad_g)
+        grad_up_ref[0] += tn(normed, grad_u)
+        grad_down_ref[0] += tn(scaled, cotangent)
+
+
+def weights_call(begin, count, first, normed, cotangent, gates, gate_w, up_w, down_w, earlier):
+    rows, width = normed.shape
+    experts = gates.shape[1]
+    hidden = gate_w.shape[2]
+    tile = 1024
+    pick = lambda e, c: (e + begin, 0, 0)
+    in_specs = [
+        pl.BlockSpec(memory_space=pltpu.SMEM),
+        pl.BlockSpec((tile, width), lambda e, c: (c, 0)),
+        pl.BlockSpec((tile, width), lambda e, c: (c, 0)),
+        pl.BlockSpec((tile, experts), lambda e, c: (c, 0)),
+        pl.BlockSpec((1, width, hidden), pick),
+        pl.BlockSpec((1, width, hidden), pick),
+        pl.BlockSpec((1, hidden, width), pick),
+    ]
+    operands = [first + begin, normed, cotangent, gates, gate_w, up_w, down_w]
+    aliases = {}
+    if earlier is not None:
+        in_specs += [pl.BlockSpec(memory_space=pl.ANY)] * 3
+        aliases = {7: 0, 8: 1, 9: 2}
+        operands += list(earlier)
+    return pl.pallas_call(
+        weights_kernel,
+        out_shape=(
+            jax.ShapeDtypeStruct(gate_w.shape, jnp.float32),
+            jax.ShapeDtypeStruct(up_w.shape, jnp.float32),
+            jax.ShapeDtypeStruct(down_w.shape, jnp.float32),
+        ),
+        grid=(count, rows // tile),
+        in_specs=in_specs,
+        out_specs=(
+            pl.BlockSpec((1, width, hidden), pick),
+            pl.BlockSpec((1, width, hidden), pick),
+            pl.BlockSpec((1, hidden, width), pick),
+        ),
+        input_output_aliases=aliases,
+        compiler_params=pltpu.CompilerParams(vmem_limit_bytes=62 << 20),
+        name="experts_weights",
+        cost_estimate=pl.CostEstimate(
+            flops=12 * rows * width * hidden * count,
+            bytes_accessed=count * (4 * rows * width + 18 * width * hidden),
+            transcendentals=0,
+        ),
+    )(*operands)
 
 
 def per_device(
@@ -100,11 +341,8 @@
         lax.all_gather(w_out, "fsdp", axis=1, tiled=True),
         lax.all_gather(norm2_gain, "fsdp", axis=0, tiled=True),
         lax.all_gather(w_router, "fsdp", axis=0, tiled=True),
-        lax.all_gather(w_gate, "fsdp", axis=0, tiled=True),
-        lax.all_gather(w_up, "fsdp", axis=0, tiled=True),
-        lax.all_gather(w_down, "fsdp", axis=0, tiled=True),
-    )
-    gain_one_b, query_w, key_w, value_w, out_w, gain_two_b, router_w, gate_w, up_w, down_w = weights
+    )
+    gain_one_b, query_w, key_w, value_w, out_w, gain_two_b, router_w = weights
     rows = tokens[0].astype(jnp.float32)
     block_len = rows.shape[0]
     heads_here = query_w.shape[1] // HEAD_DIMENSION
@@ -187,45 +425,31 @@
     scale_two = rms_scale(hidden)
     normed_two = (hidden * scale_two * gain_two_b.astype(jnp.float32)).astype(jnp.bfloat16)
     experts = router_w.shape[1]
-    logits = jnp.dot(normed_two, router_w, preferred_element_type=jnp.float32)
-    routes = expert_ids[0]
-    chooser = (routes[:, :, None] == jnp.arange(experts, dtype=jnp.int32)[None, None, :]).astype(
-        jnp.float32
-    )
-    chosen = jnp.sum(chooser * logits[:, None, :], axis=-1)
-    gates = jax.nn.softmax(chosen, axis=-1)
-    place, source, filled = slot_table(routes, experts, CAP)
+    width_all = rows.shape[1]
+    experts_here = w_gate.shape[0]
+    first = (lax.axis_index("fsdp") * experts_here).reshape(1)
+    cotangent_here = lax.all_gather(grad_output[0], "fsdp", axis=0, tiled=True)
+    cotangent_all = lax.all_gather(cotangent_here, "context", axis=0, tiled=True)
+    ids_here = lax.all_gather(expert_ids[0], "fsdp", axis=0, tiled=True)
+    ids_all = lax.all_gather(ids_here, "context", axis=0, tiled=True)
     grad_rows_out = grad_output[0].astype(jnp.float32)
-    dispatched = jnp.where(
-        filled[:, None], normed_two[source], jnp.zeros((), jnp.bfloat16)
-    ).reshape(experts, CAP, -1)
-    slot_gate = jnp.zeros((experts * CAP,), jnp.float32).at[place].set(gates.reshape(-1))
-    grad_expert = (
-        jnp.where(filled[:, None], grad_rows_out[source] * slot_gate[:, None], 0.0)
-        .astype(jnp.bfloat16)
-        .reshape(experts, CAP, -1)
-    )
-    expert_out, grad_disp, grad_gate_w, grad_up_w, grad_down_w = expert_pass(
-        dispatched, grad_expert, gate_w, up_w, down_w
-    )
-    picked = expert_out.reshape(experts * CAP, -1)[place].reshape(block_len, TOPK, -1)
-    moe_part = jnp.sum(gates[:, :, None] * picked, axis=1)
-    grad_gates_part = jnp.sum(picked * grad_rows_out[:, None, :], axis=-1)
-    grad_normed_part = jnp.sum(
-        grad_disp.reshape(experts * CAP, -1)[place].reshape(block_len, TOPK, -1), axis=1
-    )
-    moe, grad_gates, grad_normed_e = (
-        lax.psum(moe_part.astype(jnp.bfloat16), "tensor").astype(jnp.float32),
-        lax.psum(grad_gates_part.astype(jnp.bfloat16), "tensor").astype(jnp.float32),
-        lax.psum(grad_normed_part.astype(jnp.bfloat16), "tensor").astype(jnp.float32),
-    )
+    normed_here = lax.all_gather(normed_two, "fsdp", axis=0, tiled=True)
+    normed_all = lax.all_gather(normed_here, "context", axis=0, tiled=True)
+    moe_part, grad_normed_part, grad_router = own_call(
+        first, normed_here, cotangent_here, ids_here, router_w, w_gate, w_up, w_down
+    )
+    both = lax.psum_scatter(
+        jnp.stack([grad_normed_part, moe_part], axis=1), "fsdp", scatter_dimension=0, tiled=True
+    )
+    both = lax.psum(both, "tensor").astype(jnp.float32)
+    grad_normed_two, moe = both[:, 0], both[:, 1]
+    gates_all = gates_call(normed_all, ids_all, router_w)
+    expert_grads = None
+    for e in range(experts_here):
+        expert_grads = weights_call(
+            e, 1, first, normed_all, cotangent_all, gates_all, w_gate, w_up, w_down, expert_grads
+        )
     output = (hidden + moe).astype(jnp.bfloat16)
-    grad_chosen = gates * (grad_gates - jnp.sum(gates * grad_gates, axis=-1, keepdims=True))
-    grad_logits = jnp.sum(grad_chosen[:, :, None] * chooser, axis=1).astype(jnp.bfloat16)
-    grad_normed_two = grad_normed_e + jnp.dot(
-        grad_logits, router_w.T, preferred_element_type=jnp.float32
-    )
-    grad_router = jnp.dot(normed_two.T, grad_logits, preferred_element_type=jnp.float32)
     grad_hidden_n, grad_gain_two = norm_backward(
         hidden, scale_two, gain_two_b.astype(jnp.float32), grad_normed_two
     )
@@ -368,15 +592,6 @@
         lax.psum_scatter(
             grad_router.astype(jnp.bfloat16), "fsdp", scatter_dimension=0, tiled=True
         ).astype(jnp.float32),
-        lax.psum_scatter(
-            grad_gate_w.astype(jnp.bfloat16), "fsdp", scatter_dimension=0, tiled=True
-        ).astype(jnp.float32),
-        lax.psum_scatter(
-            grad_up_w.astype(jnp.bfloat16), "fsdp", scatter_dimension=0, tiled=True
-        ).astype(jnp.float32),
-        lax.psum_scatter(
-            grad_down_w.astype(jnp.bfloat16), "fsdp", scatter_dimension=0, tiled=True
-        ).astype(jnp.float32),
     )
     summed = (
         lax.psum(parts[0].astype(jnp.bfloat16), "context").astype(jnp.float32),
@@ -385,10 +600,7 @@
         lax.psum(parts[3].astype(jnp.bfloat16), "context").astype(jnp.float32),
         lax.psum(parts[4].astype(jnp.bfloat16), "context").astype(jnp.float32),
         lax.psum(parts[5].astype(jnp.bfloat16), "context").astype(jnp.float32),
-        lax.psum(parts[6].astype(jnp.bfloat16), "context").astype(jnp.float32),
-        lax.psum(parts[7].astype(jnp.bfloat16), "context").astype(jnp.float32),
-        lax.psum(parts[8].astype(jnp.bfloat16), "context").astype(jnp.float32),
-        lax.psum(parts[9].astype(jnp.bfloat16), "context").astype(jnp.float32),
+        lax.psum(parts[6].astype(jnp.bfloat16), ("context", "tensor")).astype(jnp.float32),
     )
     return (
         output[None],
@@ -400,9 +612,9 @@
         summed[4],
         summed[5],
         summed[6],
-        summed[7],
-        summed[8],
-        summed[9],
+        expert_grads[0],
+        expert_grads[1],
+        expert_grads[2],
     )
 
 

time: 1940 us -> 1260 us (0.65)
  waiting for transfers between devices: 1390 us -> 714 us
  Pallas kernels: 0 us -> 225 us
  matrix products: 202 us -> 44 us
  local copies, waits for them, and re-layouts: 129 us -> 28.6 us
  blocking collectives: 116 us -> 176 us
  other arithmetic: 71.4 us -> 42.3 us
    psum x1, waiting for transfers between devices: 492 us -> 0.01 us  [per_device(): lax.psum(parts[1].astype(jnp.bfloat16), 'context').astype(jnp.float32)]
    reduce_scatter x3 -> x2, waiting for transfers between devices: 421 us -> 59 us  [the longest x1 59 us: per_device(): lax.psum_scatter(jnp.stack([grad_normed_part, moe_part], axis=1), 'fsdp',...]
    pallas_call x0 -> x8, Pallas kernels: none -> 225 us  [the longest x6 169 us: weights_call(): pl.pallas_call(weights_kernel, out_shape=(jax.ShapeDtypeStruct(gate_w.sha...]
    all_gather x3 -> x4, waiting for transfers between devices: 309 us -> 466 us  [the longest x1 220 us: per_device(): normed_all = lax.all_gather(normed_here, 'context', axis=0, tiled=True)]
    dot_general x12 -> x0, matrix products: 142 us -> none  [the longest x1 21.2 us: expert_pass(): jnp.einsum('ecf,edf->ecd', grad_u, up_w, preferred_element_type=jnp.float32)]
    gather x4 -> x0, local copies, waits for them, and re-layouts: 71.9 us -> none  [the longest x1 20.9 us: per_device(): expert_out.reshape(experts * CAP, -1)[place].reshape(block_len, TOPK, -1)]
    all_gather x0 -> x2, blocking collectives: none -> 45.6 us  [the longest x1 38 us: per_device(): ids_all = lax.all_gather(ids_here, 'context', axis=0, tiled=True)]
    psum x1, waiting for transfers between devices: 7.15 us -> 45.5 us  [per_device(): lax.psum(jnp.dot(attended_batch, out_w, preferred_element_type=jnp.float3...]
  transfers between devices with their start and end apart: 18 -> 17, of which waited for: 14 -> 11; matrix products, arithmetic and copies ran while one was open for 13% -> 5% of each run, Pallas kernels for 0% -> 15%
where the time goes in v1:
time: 1260 us; the launch traced here: 1250 us
  waiting for transfers between devices  714 us (57%)
  Pallas kernels  225 us (18%)
  blocking collectives  176 us (14%)
  matrix products  44 us (3%)
  other arithmetic  42.3 us (3%)
  local copies, waits for them, and re-layouts  28.6 us (2%)
  between operations  15.7 us (1%)
    all_gather x1, waiting for transfers between devices, per_device(): normed_all = lax.all_gather(normed_here, 'context', axis=0, tiled=True)  220 us
    all_gather x1, waiting for transfers between devices, per_device(): lax.all_gather(cotangent_here, 'context', axis=0, tiled=True)  206 us
    pallas_call x6, Pallas kernels, weights_call(): pl.pallas_call(weights_kernel, out_shape=(jax.ShapeDtypeStruct(gate_w.sha...  169 us
    reduce_scatter x1, waiting for transfers between devices, per_device(): lax.psum_scatter(jnp.stack([grad_normed_part, moe_part], axis=1), 'fsdp',...  59 us
    psum x1, waiting for transfers between devices, per_device(): both = lax.psum(both, 'tensor').astype(jnp.float32)  53.5 us
    psum x1, waiting for transfers between devices, per_device(): lax.psum(jnp.dot(attended_batch, out_w, preferred_element_type=jnp.float3...  45.5 us
    pallas_call x1, Pallas kernels, own_call(): pl.pallas_call(own_kernel, out_shape=(jax.ShapeDtypeStruct((rows, width),...  43.4 us
    all_gather x1, blocking collectives, per_device(): ids_all = lax.all_gather(ids_here, 'context', axis=0, tiled=True)  38 us
  transfers between devices with their start and end apart: 17, of which 11 were waited for; matrix products, arithmetic and copies ran while one was open for 5% of the time, Pallas kernels for 15%

profile of v1, /device:TPU:0, one launch (start us, length us, event | category | flops | bytes accessed | tf_op | source)
XLA Modules:
  0.0 1246.4 jit_solution(9734714407605039026)
XLA Ops:
  18.3 13.7 %all_gather.48 = bf16[1536,256]{1,0:T(8,128)(2,1)S(1)} all-gather(bf16[384,256]{1,0:T(8,128)(2,1)} %param.23), channel_id=1, replica_groups=mesh['fsdp'=4,'context'=4,'tensor'=2] {'fsdp'}, dimensions={0}, use_global_device_ids=true | all-gather | bytes 983040 | tf_op jit(solution)/shard_map/all_gather | solution.py:339
  45.0 16.0 %all_gather.52 = bf16[1024,256]{1,0:T(8,128)(2,1)S(1)} all-gather(bf16[256,256]{1,0:T(8,128)(2,1)S(1)} %convolution_convert_fusion.5), channel_id=1, replica_groups=mesh['fsdp'=4,'context'=4,'tensor'=2] {'context'}, dimensions={0}, use_global_device_ids=true | all-gather | bytes 655360 | tf_op jit(solution)/shard_map/all_gather | solution.py:387
  64.5 16.0 %all_gather.49 = bf16[1024,256]{0,1:T(8,128)(2,1)S(1)} all-gather(bf16[256,256]{0,1:T(8,128)(2,1)S(1)} %bitcast.288), channel_id=1, replica_groups=mesh['fsdp'=4,'context'=4,'tensor'=2] {'context'}, dimensions={0}, use_global_device_ids=true | all-gather | bytes 655360 | tf_op jit(solution)/shard_map/all_gather | solution.py:386
  88.0 14.6 %while.28 = (s32[]{:T(128)}, f32[4,3,256]{2,1,0:T(4,128)S(1)}, f32[4,3,256]{2,1,0:T(4,128)S(1)}, f32[256,4,3,64]{0,3,2,1:T(8,128)}, s32[2]{0:T(128)S(1)}, /*inde...) while((s32[]{:T(128)}, f32[4,3,256]{2,1,0:T(4,128)S(1)}, ...), condition=%wide.region_4.5_spmd.clone, body=%wide.region_1.4_spmd.clone.sunk | while | flops 423840512 | bytes 24197304 | solution.py:418
  113.9 45.5 %all-reduce.10.cloned.1.call-done = f32[256,1536]{1,0:T(8,128)} async-done(((f32[256,1536]{1,0:T(8,128)}), f32[256,1536]{1,0:T(8,128)}) %all-reduce.10.cloned.1.call-update) | async-done | bytes 1572880 | tf_op jit(solution)/shard_map/psum | solution.py:423
  191.5 30.5 %all-gather.17.cloned.1.call-done.normed_ref = bf16[1024,1536]{1,0:T(8,128)(2,1)} async-done(((bf16[256,1536]{1,0:T(8,128)(2,1)}), bf16[1024,1536]{1,0:T(8,128)(2,1)}) %all-gather.17.cloned.1.call-update) | async-done | bytes 3145744 | tf_op jit(solution)/shard_map/all_gather | solution.py:436
  222.0 43.4 %experts_own.1 = (bf16[1024,1536]{1,0:T(8,128)(2,1)}, bf16[1024,1536]{1,0:T(8,128)(2,1)}, f32[1536,24]{1,0:T(8,128)}) custom-call(s32[1]{0:T(128)} %bitcast.13.first_ref, bf16[1024,1536]{1,0:T(8,128)(2,1)} %all-gather.17.cloned.1.call-done.normed_ref, bf16[1024,1536]{1,0:T(8,128)(2,1)} %bitcast.273, s32[1024,8]{1,0:T(8,128)} %bitcast.277, ...), custom_call_target="tpu_custom_call" | custom-call | flops 28991029248 | bytes 26738688 | tf_op jit(solution)/shard_map/experts_own/pallas_call | solution.py:216
  271.6 59.0 %reduce-scatter.10.cloned.1.call-done = bf16[256,2,1536]{2,0,1:T(8,128)(2,1)} async-done(((bf16[1024,2,1536]{2,0,1:T(8,128)(2,1)}), bf16[256,2,1536]{2,0,1:T(8,128)(2,1)}) %reduce-scatter.10.cloned.1.call-update) | async-done | bytes 1572880 | tf_op jit(solution)/shard_map/reduce_scatter | solution.py:441
  330.9 53.5 %all-reduce.12.cloned.1.call-done = bf16[256,2,1536]{2,0,1:T(8,128)(2,1)} async-done(((bf16[256,2,1536]{2,0,1:T(8,128)(2,1)}), bf16[256,2,1536]{2,0,1:T(8,128)(2,1)}) %all-reduce.12.cloned.1.call-update) | async-done | bytes 1572880 | tf_op jit(solution)/shard_map/psum | solution.py:444
  393.2 21.6 %while.29 = (s32[]{:T(128)}, f32[256,4,3,64]{0,3,2,1:T(8,128)S(1)}, bf16[2,512,512]{2,1,0:T(8,128)(2,1)}, bf16[2,512,4,64]{1,3,2,0:T(8,128)(2,1)S(1)}, s32[2]{0:...) while((s32[]{:T(128)}, f32[256,4,3,64]{0,3,2,1:T(8,128)S(1)}, ...), condition=%wide.region_12.13_spmd.clone, body=%wide.region_11.12_spmd.clone.sunk | while | flops 1024393984 | bytes 38455500 | solution.py:528
  420.7 21.6 %reduce-scatter.12.cloned.1.call-done = bf16[256,512]{1,0:T(8,128)(2,1)} async-done(((bf16[1024,512]{1,0:T(8,128)(2,1)}), bf16[256,512]{1,0:T(8,128)(2,1)}) %reduce-scatter.12.cloned.1.call-update) | async-done | bytes 262160 | tf_op jit(solution)/shard_map/reduce_scatter | solution.py:531
  463.7 38.0 %all-gather.3 = s32[1,4096,8]{2,1,0:T(8,128)} all-gather(s32[1,1024,8]{2,1,0:T(8,128)S(1)} %copy-done.16), channel_id=5, replica_groups=mesh['fsdp'=4,'context'=4,'tensor'=2] {'context'}, dimensions={1}, use_global_device_ids=true | all-gather | bytes 163840 | tf_op jit(solution)/shard_map/all_gather | solution.py:434
  501.7 36.9 %psum.79 = bf16[384,24]{1,0:T(8,128)(2,1)S(1)} all-reduce(bf16[384,24]{1,0:T(8,128)(2,1)} %reduce-scatter.20.cloned.1.call-done), channel_id=1, replica_groups=mesh['fsdp'=4,'context'=4,'tensor'=2] {'context','tensor'}, use_global_device_ids=true, to_apply=%region_31.32 | all-reduce | flops 9216 | bytes 36864 | tf_op jit(solution)/shard_map/psum | solution.py:603
  564.0 26.4 %reduce-scatter.16.cloned.1.call-done = bf16[384,256]{1,0:T(8,128)(2,1)} async-done(((bf16[1536,256]{1,0:T(8,128)(2,1)}), bf16[384,256]{1,0:T(8,128)(2,1)}) %reduce-scatter.16.cloned.1.call-update) | async-done | bytes 196624 | tf_op jit(solution)/shard_map/reduce_scatter | solution.py:580
  590.4 35.8 %reduce-scatter.14.cloned.1.call-done = bf16[384,768]{1,0:T(8,128)(2,1)} async-done(((bf16[1536,768]{1,0:T(8,128)(2,1)}), bf16[384,768]{1,0:T(8,128)(2,1)}) %reduce-scatter.14.cloned.1.call-update) | async-done | bytes 589840 | tf_op jit(solution)/shard_map/reduce_scatter | solution.py:577
  626.2 219.6 %all-gather.19.cloned.1.call-done.normed_ref.refs_0_ = bf16[4096,1536]{1,0:T(8,128)(2,1)} async-done(((bf16[1024,1536]{1,0:T(8,128)(2,1)}), bf16[4096,1536]{1,0:T(8,128)(2,1)}) %all-gather.19.cloned.1.call-update) | async-done | bytes 12582928 | tf_op jit(solution)/shard_map/all_gather | solution.py:437
  845.8 12.2 gates_all.1.refs_2_
  858.0 205.6 %all-gather.23.cloned.1.call-done = bf16[1,4096,1536]{2,1,0:T(8,128)(2,1)} async-done(((bf16[1,1024,1536]{2,1,0:T(8,128)(2,1)}), bf16[1,4096,1536]{2,1,0:T(8,128)(2,1)}) %all-gather.23.cloned.1.call-update) | async-done | bytes 12582928 | tf_op jit(solution)/shard_map/all_gather | solution.py:432
  1063.7 28.8 %experts_weights.6 = (f32[6,1536,256]{2,1,0:T(8,128)}, f32[6,1536,256]{2,1,0:T(8,128)}, f32[6,256,1536]{2,1,0:T(8,128)}) custom-call(s32[1]{0:T(128)} %bitcast.13.first_ref, bf16[4096,1536]{1,0:T(8,128)(2,1)} %all-gather.19.cloned.1.call-done.normed_ref.refs_0_, bf16[4096,1536]{1,0:T(8,128)(2,1)} %bitcast.291, f32[4096,24]{1,0:T(8,128)} %gates_all.1.refs_2_, ...), custom_call_target="tpu_custom_call" | custom-call | flops 19327352832 | bytes 32243712 | tf_op jit(solution)/shard_map/experts_weights/pallas_call | solution.py:295
  1092.5 28.1 %experts_weights.7 = (f32[6,1536,256]{2,1,0:T(8,128)}, f32[6,1536,256]{2,1,0:T(8,128)}, f32[6,256,1536]{2,1,0:T(8,128)}) custom-call(s32[1]{0:T(128)S(6)} %add.168.first_ref, bf16[4096,1536]{1,0:T(8,128)(2,1)} %all-gather.19.cloned.1.call-done.normed_ref.refs_0_, ...), custom_call_target="tpu_custom_call", output_to_operand_aliasing={{0}: (7, {}), {1}: (8, {}), {2}: (9, {})} | custom-call | flops 19327352832 | bytes 32243712 | tf_op jit(solution)/shard_map/experts_weights/pallas_call | solution.py:295
  1120.6 27.9 %experts_weights.8 = (f32[6,1536,256]{2,1,0:T(8,128)}, f32[6,1536,256]{2,1,0:T(8,128)}, f32[6,256,1536]{2,1,0:T(8,128)}) custom-call(s32[1]{0:T(128)S(6)} %add.167.first_ref, bf16[4096,1536]{1,0:T(8,128)(2,1)} %all-gather.19.cloned.1.call-done.normed_ref.refs_0_, ...), custom_call_target="tpu_custom_call", output_to_operand_aliasing={{0}: (7, {}), {1}: (8, {}), {2}: (9, {})} | custom-call | flops 19327352832 | bytes 32243712 | tf_op jit(solution)/shard_map/experts_weights/pallas_call | solution.py:295
  1148.5 28.1 %experts_weights.9 = (f32[6,1536,256]{2,1,0:T(8,128)}, f32[6,1536,256]{2,1,0:T(8,128)}, f32[6,256,1536]{2,1,0:T(8,128)}) custom-call(s32[1]{0:T(128)S(6)} %add.166.first_ref, bf16[4096,1536]{1,0:T(8,128)(2,1)} %all-gather.19.cloned.1.call-done.normed_ref.refs_0_, ...), custom_call_target="tpu_custom_call", output_to_operand_aliasing={{0}: (7, {}), {1}: (8, {}), {2}: (9, {})} | custom-call | flops 19327352832 | bytes 32243712 | tf_op jit(solution)/shard_map/experts_weights/pallas_call | solution.py:295
  1176.6 27.9 %experts_weights.10 = (f32[6,1536,256]{2,1,0:T(8,128)}, f32[6,1536,256]{2,1,0:T(8,128)}, f32[6,256,1536]{2,1,0:T(8,128)}) custom-call(s32[1]{0:T(128)S(6)} %add.165.first_ref, bf16[4096,1536]{1,0:T(8,128)(2,1)} %all-gather.19.cloned.1.call-done.normed_ref.refs_0_, ...), custom_call_target="tpu_custom_call", output_to_operand_aliasing={{0}: (7, {}), {1}: (8, {}), {2}: (9, {})} | custom-call | flops 19327352832 | bytes 32243712 | tf_op jit(solution)/shard_map/experts_weights/pallas_call | solution.py:295
  1204.5 28.2 %experts_weights.11 = (f32[6,1536,256]{2,1,0:T(8,128)}, f32[6,1536,256]{2,1,0:T(8,128)}, f32[6,256,1536]{2,1,0:T(8,128)}) custom-call(s32[1]{0:T(128)S(6)} %add.164.first_ref, bf16[4096,1536]{1,0:T(8,128)(2,1)} %all-gather.19.cloned.1.call-done.normed_ref.refs_0_, ...), custom_call_target="tpu_custom_call", output_to_operand_aliasing={{0}: (7, {}), {1}: (8, {}), {2}: (9, {})} | custom-call | flops 19327352832 | bytes 32243712 | tf_op jit(solution)/shard_map/experts_weights/pallas_call | solution.py:295
  (250 shorter events, 187.6 us)
Async XLA Ops:
  7.2 37.0 %copy-start.4 = (bf16[1,256,1536]{2,1,0:T(8,128)(2,1)S(1)}, bf16[1,256,1536]{2,1,0:T(8,128)(2,1)}, u32[]{:S(2)}) copy-start(bf16[1,256,1536]{2,1,0:T(8,128)(2,1)} %param.18) | copy-start | bytes 2359300
  7.2 73.8 %all-gather.13.cloned.1.call-start = ((), (), s32[]{:S(2)}) async-start(), calls=%async_computation.7 | async-start | bytes 2949120 | tf_op jit(solution)/shard_map/all_gather | solution.py:338
  7.9 96.5 %all-gather.15.cloned.1.call-start = ((), (), s32[]{:S(2)}) async-start(), calls=%async_computation.8 | async-start | bytes 2949120 | tf_op jit(solution)/shard_map/all_gather | solution.py:341
  8.7 150.8 %all-reduce.10.cloned.1.call-start = ((), (), s32[]{:S(2)}) async-start(), calls=%async_computation.9 | async-start | bytes 3145728 | tf_op jit(solution)/shard_map/psum | solution.py:423
  11.4 73.8 %copy-start.31 = (f32[256]{0:T(256)}, f32[256]{0:T(256)S(1)}, u32[]{:S(2)}) copy-start(f32[256]{0:T(256)S(1)} %get-tuple-element.406) | copy-start | bytes 3076
  18.3 67.0 %copy-start.28 = (f32[1536]{0:T(1024)}, f32[1536]{0:T(1024)S(1)}, u32[]{:S(2)}) copy-start(f32[1536]{0:T(1024)S(1)} %reshape.300) | copy-start | bytes 18436
  32.0 30.8 %copy-start.8 = (bf16[1536,256]{1,0:T(8,128)(2,1)}, bf16[1536,256]{1,0:T(8,128)(2,1)S(1)}, u32[]{:S(2)}) copy-start(bf16[1536,256]{1,0:T(8,128)(2,1)S(1)} %all_gather.48) | copy-start | bytes 2359300
  108.1 83.5 %all-gather.21.cloned.1.call-start = ((), (), s32[]{:S(2)}) async-start(), calls=%async_computation.20 | async-start | bytes 3932160 | tf_op jit(solution)/shard_map/all_gather | solution.py:431
  108.6 113.4 %all-gather.17.cloned.1.call-start = ((), (), s32[]{:S(2)}) async-start(), calls=%async_computation.10 | async-start | bytes 3932160 | tf_op jit(solution)/shard_map/all_gather | solution.py:436
  163.5 167.1 %reduce-scatter.10.cloned.1.call-start = ((), (), s32[]{:S(2)}) async-start(), calls=%async_computation.11 | async-start | bytes 7864320 | tf_op jit(solution)/shard_map/reduce_scatter | solution.py:441
  271.6 59.4 %copy-start.18 = (f32[4,3,256]{2,1,0:T(4,128)S(1)}, f32[4,3,256]{2,1,0:T(4,128)}, u32[]{:S(2)}) copy-start(f32[4,3,256]{2,1,0:T(4,128)} %copy-done.17) | copy-start | bytes 36868
  271.6 112.9 %all-reduce.12.cloned.1.call-start = ((), (), s32[]{:S(2)}) async-start(), calls=%async_computation.12 | async-start | bytes 3145728 | tf_op jit(solution)/shard_map/psum | solution.py:444
  330.6 111.7 %reduce-scatter.12.cloned.1.call-start = ((), (), s32[]{:S(2)}) async-start(), calls=%async_computation.13 | async-start | bytes 1310720 | tf_op jit(solution)/shard_map/reduce_scatter | solution.py:531
  414.9 86.9 %reduce-scatter.20.cloned.1.call-start = ((), (), s32[]{:S(2)}) async-start(), calls=%async_computation.18 | async-start | bytes 491520 | tf_op jit(solution)/shard_map/reduce_scatter | solution.py:592
  417.0 122.3 %all-reduce.14.cloned.1.call-start = ((), (), s32[]{:S(2)}) async-start(), calls=%async_computation.14 | async-start | bytes 1572864 | tf_op jit(solution)/shard_map/psum | solution.py:561
  418.7 27.1 %copy-start.9 = (bf16[1536,256]{1,0:T(8,128)(2,1)S(1)}, bf16[1536,256]{1,0:T(8,128)(2,1)}, u32[]{:S(2)}) copy-start(bf16[1536,256]{1,0:T(8,128)(2,1)} %copy-done.8) | copy-start | bytes 2359300
  447.6 111.8 %reduce-scatter.22.cloned.1.call-start = ((), (), s32[]{:S(2)}) async-start(), calls=%async_computation.22 | async-start | bytes 2949120
  454.3 109.7 %reduce-scatter.18.cloned.1.call-start = ((), (), s32[]{:S(2)}) async-start(), calls=%async_computation.17 | async-start | bytes 983040 | tf_op jit(solution)/shard_map/reduce_scatter | solution.py:583
  456.9 133.5 %reduce-scatter.16.cloned.1.call-start = ((), (), s32[]{:S(2)}) async-start(), calls=%async_computation.16 | async-start | bytes 983040 | tf_op jit(solution)/shard_map/reduce_scatter | solution.py:580
  458.4 167.8 %reduce-scatter.14.cloned.1.call-start = ((), (), s32[]{:S(2)}) async-start(), calls=%async_computation.15 | async-start | bytes 2949120 | tf_op jit(solution)/shard_map/reduce_scatter | solution.py:577
  461.2 384.6 %all-gather.19.cloned.1.call-start = ((), (), s32[]{:S(2)}) async-start(), calls=%async_computation.19 | async-start | bytes 15728640 | tf_op jit(solution)/shard_map/all_gather | solution.py:437
  461.8 601.9 %all-gather.23.cloned.1.call-start = ((), (), s32[]{:S(2)}) async-start(), calls=%async_computation.21 | async-start | bytes 15728640 | tf_op jit(solution)/shard_map/all_gather | solution.py:432
  462.4 94.5 %copy-start.34 = (f32[256]{0:T(256)S(1)}, f32[256]{0:T(256)}, u32[]{:S(2)}) copy-start(f32[256]{0:T(256)} %get-tuple-element.405) | copy-start | bytes 3076
  462.4 770.3 %all-reduce.16.cloned.1.call-start = ((), (), s32[]{:S(2)}) async-start(), calls=%async_computation.23 | async-start | bytes 3145728 | tf_op jit(solution)/shard_map/psum | solution.py:598
  (34 other events, 134.9 us)
Sparse Core Ops, SparseCore 0:
  9.6 34.1 all-gather.12
  45.3 23.8 all-gather.14
  108.2 51.2 all-reduce.9
  160.9 30.6 all-gather.20
  193.5 28.4 all-gather.16
  271.7 58.8 reduce-scatter.9
  332.9 51.5 all-reduce.11
  415.0 27.2 reduce-scatter.11
  445.4 19.2 reduce-scatter.19
  467.4 34.3 all-reduce.13
  504.9 32.8 reduce-scatter.21
  540.8 23.1 reduce-scatter.17
  567.1 23.2 reduce-scatter.15
  593.4 32.8 reduce-scatter.13
  627.6 218.1 all-gather.18
  847.3 216.3 all-gather.22
  1066.1 67.3 all-reduce.15
